TPU v7x, 32 devices: a whole 2x2x4 slice. The times are simulated.
32 devices in a mesh: dp: 4 (over x, core), expert: 8 (over z, y).
Axes of the slice: x: 2, y: 2, z: 4, core: 2. Of those that a mesh axis runs over, the one named last changes fastest.
Arguments:
- tokens: bfloat16 [128, 256, 1280], P(('dp', 'expert')), may hold values from -32 to 32
- slot_keys: bfloat16 [1280, 8], replicated, may hold values from -20 to 20
- logit_scale: float32 [1], replicated, may hold values from 8 to 16
- up_weight: bfloat16 [8, 1280, 5120], P('expert', None, 'dp'), may hold values from -0.15625 to 0.15625
- up_bias: bfloat16 [8, 5120], P('expert', 'dp'), may hold values from -3 to 3
- down_weight: bfloat16 [8, 5120, 1280], P('expert', 'dp'), may hold values from -0.078125 to 0.078125
- down_bias: bfloat16 [8, 1280], replicated, may hold values from -3 to 3
Outputs:
- mixed_out: bfloat16 [128, 256, 1280], P(('dp', 'expert'))
All inputs are finite; a program needn't handle non-finite values.
Results may differ from a plain program's by a relative error of at most 0.017.
Values may be sent and summed in bfloat16 or wider, within the bound.
A program may use at most 64 MiB of HBM per device.

v0:
```python
import functools

import jax
import jax.numpy as jnp
from jax import lax
from jax.experimental import pallas as pl
from jax.experimental.pallas import tpu as pltpu
from jax.sharding import PartitionSpec as P

MESH = pl.DeviceIdType.MESH
F32 = jnp.float32
BF16 = jnp.bfloat16
norm_eps = 1e-06
NT = (((1,), (1,)), ((), ()))
CORES = 2


def erf_gelu(v):
    return 0.5 * v * (1.0 + lax.erf(v * 0.7071067811865476))


def route_and_experts(
    owners,
    n_dp,
    chunk,
    tok_hbm,
    keys_hbm,
    scale_hbm,
    w1_hbm,
    b1_hbm,
    w2_hbm,
    b2_hbm,
    comb_ref,
    ret_ref,
    keys_ref,
    scale_ref,
    b1_ref,
    b2_ref,
    tok,
    w1,
    w2,
    send,
    recv,
    xf,
    hid,
    part,
    mine,
    pair,
    back,
    got,
    small_sem,
    tok_sem,
    w_sem,
    own_sem,
    s_send,
    s_recv,
    r_send,
    r_recv,
    p_send,
    p_recv,
    b_send,
    b_recv,
):
    images, patches, width = tok.shape
    hidden = w1.shape[1]
    halves = n_dp // CORES
    groups = halves * owners
    rows = groups * images
    slots = owners * images

    d = lax.axis_index("dp")
    e = lax.axis_index("expert")
    core = lax.rem(d, CORES)
    half = lax.div(d, CORES)
    me = half * owners + e
    other = 1 - core
    partner = {"dp": half * CORES + other, "expert": e}

    quarter = max(1, owners // 4)
    outward = [
        (a, q * quarter + b)
        for q in (2, 3, 1, 0)
        for b in range(quarter)
        for a in reversed(range(halves))
        if q * quarter + b < owners and (a, q * quarter + b) != (0, 0)
    ]
    inward = outward[::-1]

    def for_peers(act, order):
        if groups <= 16:
            for a, b in order:
                act(lax.rem(half + a, halves) * owners + lax.rem(e + b, owners))
        else:

            def step(k, c):
                act(lax.rem(me + k, groups))
                return c

            lax.fori_loop(1, groups, step, 0)

    def device(t):
        return {"dp": lax.div(t, owners) * CORES + core, "expert": lax.rem(t, owners)}

    load_keys = pltpu.make_async_copy(keys_hbm, keys_ref, small_sem.at[0])
    load_scale = pltpu.make_async_copy(scale_hbm, scale_ref, small_sem.at[1])
    load_b1 = pltpu.make_async_copy(b1_hbm, b1_ref, small_sem.at[2])
    load_b2 = pltpu.make_async_copy(b2_hbm, b2_ref, small_sem.at[3])
    load_keys.start()
    load_scale.start()
    for i in range(images):
        pltpu.make_async_copy(tok_hbm.at[i], tok.at[i], tok_sem.at[i]).start()
    load1 = pltpu.make_async_copy(w1_hbm.at[0], w1, w_sem.at[0])
    load2 = pltpu.make_async_copy(w2_hbm.at[0], w2, w_sem.at[1])
    barrier = pltpu.get_barrier_semaphore()
    pl.semaphore_signal(barrier, inc=1, device_id=partner, device_id_type=MESH)

    def greet(k, c):
        t = lax.rem(me + k, groups)
        pl.semaphore_signal(barrier, inc=1, device_id=device(t), device_id_type=MESH)
        return c

    lax.fori_loop(1, groups, greet, 0)

    load_keys.wait()
    keys = keys_ref[...].astype(F32)
    keys = keys * lax.rsqrt(jnp.mean(keys * keys, axis=1, keepdims=True) + norm_eps)
    slot_of = lax.broadcasted_iota(jnp.int32, (slots, owners), 0) // images
    col = lax.broadcasted_iota(jnp.int32, (slots, owners), 1)
    spread = jnp.where(slot_of == col, 1.0, 0.0).astype(BF16)
    keys = jnp.dot(spread, keys.astype(BF16), preferred_element_type=F32)
    keys = keys.astype(BF16)
    ones = jnp.ones((16, width), BF16)
    load_scale.wait()
    factor = scale_ref[0] / width
    image_of = lax.broadcasted_iota(jnp.int32, (slots, patches), 0) % images

    scores = []
    for i in range(images):
        pltpu.make_async_copy(tok_hbm.at[i], tok.at[i], tok_sem.at[i]).wait()
        t = tok[i]
        raw = lax.dot_general(keys, t, NT, preferred_element_type=F32)
        squares = lax.dot_general(ones, t * t, NT, preferred_element_type=F32)[0:1]
        scores.append(raw * (lax.rsqrt(squares / width + norm_eps) * factor))
    load1.start()
    load2.start()
    load_b1.start()
    load_b2.start()
    parts = []
    for i in range(images):
        up = jnp.exp(scores[i] - jnp.max(scores[i], axis=1, keepdims=True))
        up = up / jnp.sum(up, axis=1, keepdims=True)
        parts.append(jnp.where(image_of == i, up, 0.0).astype(BF16))
    total = jnp.zeros((slots, width), F32)
    for i in range(images):
        total = total + jnp.dot(parts[i], tok[i], preferred_element_type=F32)
    for n in range(owners):
        send[n] = total[n * images : (n + 1) * images].astype(BF16)

    pl.semaphore_wait(barrier, groups)

    def out_copy(t):
        return pltpu.make_async_remote_copy(
            src_ref=send.at[lax.rem(t, owners)],
            dst_ref=recv.at[core, me],
            send_sem=s_send.at[t],
            recv_sem=s_recv.at[me],
            device_id=device(t),
            device_id_type=MESH,
        )

    def in_copy(t):
        return pltpu.make_async_remote_copy(
            src_ref=send.at[0],
            dst_ref=recv.at[core, t],
            send_sem=s_send.at[t],
            recv_sem=s_recv.at[t],
            device_id=device(t),
            device_id_type=MESH,
        )

    def relay(side, t):
        return pltpu.make_async_remote_copy(
            src_ref=recv.at[side, t],
            dst_ref=recv.at[side, t],
            send_sem=r_send.at[t],
            recv_sem=r_recv.at[t],
            device_id=partner,
            device_id_type=MESH,
        )

    own = pltpu.make_async_copy(send.at[e], recv.at[core, me], own_sem.at[0])
    own.start()

    def start_out(t):
        out_copy(t).start()

    for_peers(start_out, outward)
    own.wait()
    relay(core, me).start()
    for i in range(images):
        mix = jnp.exp(scores[i] - jnp.max(scores[i], axis=0, keepdims=True))
        mix = mix * (images / jnp.sum(mix, axis=0, keepdims=True))
        comb_ref[i] = jnp.where(image_of == i, mix, 0.0).astype(BF16)

    def pass_on(t):
        in_copy(t).wait_recv()
        relay(core, t).start()

    for_peers(pass_on, inward)

    def take(k, c):
        relay(other, k).wait_recv()
        return c

    lax.fori_loop(0, groups, take, 0)

    for side in range(CORES):

        def place(k, c):
            pairs = [recv[side, 2 * k + q].astype(F32) for q in range(2)]
            at = pl.multiple_of(side * rows + k * 2 * images, 2 * images)
            xf[pl.ds(at, 2 * images), :] = jnp.concatenate(pairs, axis=0)
            return c

        lax.fori_loop(0, groups // 2, place, 0, unroll=groups <= 16)

    load1.wait()
    load_b1.wait()
    load_b2.wait()
    block = min(128, CORES * rows)
    steps = CORES * rows // block

    def first(m, c):
        at = pl.multiple_of(m * block, block)
        x = xf[pl.ds(at, block), :].astype(BF16)
        for j in range(0, hidden, chunk):
            v = jnp.dot(x, w1[:, j : j + chunk], preferred_element_type=F32)
            v = v + b1_ref[0:1, j : j + chunk].astype(F32)
            hid[pl.ds(at, block), j : j + chunk] = erf_gelu(v).astype(BF16)
        return c

    lax.fori_loop(0, steps, first, 0, unroll=steps == 1)
    load2.wait()

    def pair_copy(j):
        return pltpu.make_async_remote_copy(
            src_ref=part.at[j, pl.ds(pl.multiple_of(other * rows, rows), rows)],
            dst_ref=pair.at[j],
            send_sem=p_send.at[j],
            recv_sem=p_recv.at[j],
            device_id=partner,
            device_id_type=MESH,
        )

    pieces = width // chunk
    for j in range(pieces):

        def second(m, c):
            at = pl.multiple_of(m * block, block)
            h = hid[pl.ds(at, block), :]
            v = jnp.dot(h, w2[:, j * chunk : (j + 1) * chunk], preferred_element_type=F32)
            part[j, pl.ds(at, block), :] = v.astype(BF16)
            mine[j, pl.ds(at, block), :] = v
            return c

        lax.fori_loop(0, steps, second, 0, unroll=steps == 1)
        pair_copy(j).start()

    for j in range(pieces):
        pair_copy(j).wait_recv()

        def join(k, c):
            at = pl.multiple_of(k * 4 * images, 4 * images)
            own_at = pl.multiple_of(core * rows + at, 4 * images)
            v = mine[j, pl.ds(own_at, 4 * images), :]
            v = v + pair[j, pl.ds(at, 4 * images), :].astype(F32)
            for q in range(4):
                back[4 * k + q, :, j * chunk : (j + 1) * chunk] = v[
                    q * images : (q + 1) * images
                ].astype(BF16)
            return c

        lax.fori_loop(0, groups // 4, join, 0, unroll=groups <= 16)

    def home(t):
        return pltpu.make_async_remote_copy(
            src_ref=back.at[t],
            dst_ref=got.at[me],
            send_sem=b_send.at[t],
            recv_sem=b_recv.at[me],
            device_id=device(t),
            device_id_type=MESH,
        )

    def landed(t):
        return pltpu.make_async_remote_copy(
            src_ref=back.at[t],
            dst_ref=got.at[t],
            send_sem=b_send.at[t],
            recv_sem=b_recv.at[t],
            device_id=device(t),
            device_id_type=MESH,
        )

    keep_own = pltpu.make_async_copy(back.at[me], got.at[me], own_sem.at[1])
    keep_own.start()

    def start_home(t):
        home(t).start()

    for_peers(start_home, outward)

    def end_sends(k, c):
        out_copy(lax.rem(me + k, groups)).wait_send()
        return c

    lax.fori_loop(1, groups, end_sends, 0)

    def end_relays(k, c):
        relay(core, k).wait_send()
        return c

    lax.fori_loop(0, groups, end_relays, 0)
    for j in range(pieces):
        pair_copy(j).wait_send()
    keep_own.wait()

    def arrive(k, c):
        landed(lax.rem(me + groups - k, groups)).wait_recv()
        return c

    lax.fori_loop(1, groups, arrive, 0)
    bias = b2_ref[...].astype(F32)
    for n in range(0, owners, 2):
        both = []
        for q in (n, n + 1):
            v = got[q].astype(F32)
            for x in range(1, halves):
                v = v + got[x * owners + q].astype(F32)
            both.append(v + bias[q : q + 1])
        ret_ref[n * images : (n + 2) * images, :] = jnp.concatenate(both, axis=0)

    def end_home(k, c):
        home(lax.rem(me + k, groups)).wait_send()
        return c

    lax.fori_loop(1, groups, end_home, 0)


def mix_kernel(comb_ref, ret_ref, out_ref, out, out_sem):
    images = comb_ref.shape[0]
    ret = ret_ref[...].astype(BF16)
    copies = []
    for i in range(images):
        v = lax.dot_general(
            comb_ref[i], ret, (((0,), (0,)), ((), ())), preferred_element_type=F32
        )
        out[i] = v.astype(out.dtype)
        copies.append(pltpu.make_async_copy(out.at[i], out_ref.at[i], out_sem.at[i]))
        copies[-1].start()
    for copy in copies:
        copy.wait()


def body(tokens, slot_keys, logit_scale, up_weight, up_bias, down_weight, down_bias):
    images, patches, width = tokens.shape
    owners = lax.axis_size("expert")
    n_dp = lax.axis_size("dp")
    hidden = up_weight.shape[2]
    halves = n_dp // CORES
    groups = halves * owners
    rows = groups * images
    slots = owners * images
    chunk = 256
    pieces = width // chunk
    vmem = pl.BlockSpec(memory_space=pltpu.VMEM)
    hbm = pl.BlockSpec(memory_space=pl.ANY)
    dma = pltpu.SemaphoreType.DMA
    comb, ret = pl.pallas_call(
        functools.partial(route_and_experts, owners, n_dp, chunk),
        out_shape=(
            pltpu.VMEM((images, slots, patches), BF16),
            pltpu.VMEM((slots, width), F32),
        ),
        in_specs=[
            hbm,
            hbm,
            pl.BlockSpec(memory_space=pltpu.HBM),
            hbm,
            hbm,
            hbm,
            hbm,
        ],
        out_specs=(vmem, vmem),
        scratch_shapes=[
            pltpu.VMEM((owners, width), BF16),
            pltpu.SMEM((1,), F32),
            pltpu.VMEM(up_bias.shape, BF16),
            pltpu.VMEM(down_bias.shape, BF16),
            pltpu.VMEM((images, patches, width), BF16),
            pltpu.VMEM((width, hidden), BF16),
            pltpu.VMEM((hidden, width), BF16),
            pltpu.VMEM((owners, images, width), BF16),
            pltpu.VMEM((CORES, groups, images, width), BF16),
            pltpu.VMEM((CORES * rows, width), F32),
            pltpu.VMEM((CORES * rows, hidden), BF16),
            pltpu.VMEM((pieces, CORES * rows, chunk), BF16),
            pltpu.VMEM((pieces, CORES * rows, chunk), F32),
            pltpu.VMEM((pieces, rows, chunk), BF16),
            pltpu.VMEM((groups, images, width), BF16),
            pltpu.VMEM((groups, images, width), BF16),
            dma((4,)),
            dma((images,)),
            dma((2,)),
            dma((2,)),
            dma((groups,)),
            dma((groups,)),
            dma((groups,)),
            dma((groups,)),
            dma((pieces,)),
            dma((pieces,)),
            dma((groups,)),
            dma((groups,)),
        ],
        compiler_params=pltpu.CompilerParams(
            collective_id=0, has_side_effects=True, vmem_limit_bytes=60 * 1024 * 1024
        ),
        name="route_and_experts",
    )(tokens, slot_keys.T, logit_scale, up_weight, up_bias, down_weight, down_bias)
    return pl.pallas_call(
        mix_kernel,
        out_shape=jax.ShapeDtypeStruct(tokens.shape, BF16),
        in_specs=[vmem, vmem],
        out_specs=hbm,
        scratch_shapes=[pltpu.VMEM(tokens.shape, BF16), dma((images,))],
        name="mix_tokens",
    )(
        pltpu.with_memory_space_constraint(comb, pltpu.VMEM),
        pltpu.with_memory_space_constraint(ret, pltpu.VMEM),
    )


def solution(mesh):
    return jax.shard_map(
        body,
        mesh=mesh,
        in_specs=(
            P(("dp", "expert"), None, None),
            P(),
            P(),
            P("expert", None, "dp"),
            P("expert", "dp"),
            P("expert", "dp", None),
            P(),
        ),
        out_specs=P(("dp", "expert"), None, None),
        check_vma=False,
    )
```

profile of v0, /device:TPU:0, one launch (start us, length us, event | category | flops | bytes accessed | tf_op | source)
XLA Modules:
  0.0 26.7 jit_solution(14630952298551950206)
XLA Ops:
  0.7 24.1 %route_and_experts.1 = (bf16[4,32,256]{2,1,0:T(8,128)(2,1)S(1)}, f32[32,1280]{1,0:T(8,128)S(1)}) custom-call(bf16[4,256,1280]{2,1,0:T(8,128)(2,1)} %tok_hbm.1, bf16[8,1280]{1,0:T(8,128)(2,1)} %bitcast.1, f32[1]{0:T(128)S(6)} %copy.8.scale_hbm, bf16[1,1280,1280]{2,1,0:T(8,128)(2,1)} %w1_hbm.1, bf16[1,1280]{1,0:T(2,128)(2,1)} %b1_hbm.1, ...), custom_call_target="tpu_custom_call" | custom-call | tf_op jit(solution)/shard_map/route_and_experts/pallas_call | solution.py:379
  24.8 1.9 %mix_tokens.1 = bf16[4,256,1280]{2,1,0:T(8,128)(2,1)} custom-call(bf16[4,32,256]{2,1,0:T(8,128)(2,1)S(1)} %get-tuple-element.7.comb_ref, f32[32,1280]{1,0:T(8,128)S(1)} %get-tuple-element.8.ret_ref), custom_call_target="tpu_custom_call" | custom-call | tf_op jit(solution)/shard_map/mix_tokens/pallas_call | solution.py:430
where the time goes:
time: 26.9 us; the launch traced here: 26.7 us
  Pallas kernels  26 us (97%)
  between operations  0.66 us (2%)
    pallas_call x1, Pallas kernels, body(): pl.pallas_call(functools.partial(route_and_experts, owners, n_dp, chunk),...  24.1 us
    pallas_call x1, Pallas kernels, body(): pl.pallas_call(mix_kernel, out_shape=jax.ShapeDtypeStruct(tokens.shape, B...  1.9 us

commit v1 on v0

v1 whole, which is shorter than its diff:
```python
import functools

import jax
import jax.numpy as jnp
from jax import lax
from jax.experimental import pallas as pl
from jax.experimental.pallas import tpu as pltpu
from jax.sharding import PartitionSpec as P

MESH = pl.DeviceIdType.MESH
F32 = jnp.float32
BF16 = jnp.bfloat16
norm_eps = 1e-06
NT = (((1,), (1,)), ((), ()))
CORES = 2
BANDS = 4
LOG2E = 1.4426950408889634


def erf_gelu(v):
    return 0.5 * v * (1.0 + lax.erf(v * 0.7071067811865476))


def row_squares(t):
    patches, width = t.shape
    s = jnp.zeros((patches, 128), F32)
    for j in range(0, width, 128):
        u = t[:, j : j + 128].astype(F32)
        s = s + u * u
    hi = s.astype(BF16)
    lo = (s - hi.astype(F32)).astype(BF16)
    both = jnp.concatenate([hi, lo], axis=1)
    ones = jnp.ones((16, 256), BF16)
    return lax.dot_general(ones, both, NT, preferred_element_type=F32)[0:1]


def route_and_experts(
    owners,
    n_dp,
    chunk,
    cuts,
    tok_hbm,
    keys_hbm,
    scale_hbm,
    w1_hbm,
    b1_hbm,
    w2_hbm,
    b2_hbm,
    comb_ref,
    ret_ref,
    keys_ref,
    scale_ref,
    b1_ref,
    b2_ref,
    tok,
    w1,
    w2,
    send,
    recv,
    xf,
    hid,
    part,
    mine,
    pair,
    back,
    got,
    load_sem,
    tok_sem,
    sent_sem,
    band_sem,
    land_sem,
    p_recv,
):
    images, patches, width = tok.shape
    hidden = w1.shape[1]
    halves = n_dp // CORES
    groups = halves * owners
    per = groups // BANDS
    rows = groups * images
    slots = owners * images

    d = lax.axis_index("dp")
    e = lax.axis_index("expert")
    core = lax.rem(d, CORES)
    half = lax.div(d, CORES)
    me = e * halves + half
    band = lax.div(e, owners // BANDS)
    other = 1 - core
    partner = {"dp": half * CORES + other, "expert": e}

    low = band < BANDS // 2
    near = [
        band,
        band + 1 - 2 * lax.rem(band, 2),
        jnp.where(low, 2, 1),
        jnp.where(low, 3, 0),
    ]

    def for_band(act, b):
        if per <= 8:
            for m in range(per):
                ee = b * (per // halves) + m // halves
                dev = {"dp": (m % halves) * CORES + other, "expert": ee}
                act(b * per + m, dev)
        else:

            def step(m, c):
                t = b * per + m
                dev = {
                    "dp": lax.rem(t, halves) * CORES + other,
                    "expert": lax.div(t, halves),
                }
                act(t, dev)
                return c

            lax.fori_loop(0, per, step, 0)

    load_keys = pltpu.make_async_copy(keys_hbm, keys_ref, load_sem.at[0])
    load_scale = pltpu.make_async_copy(scale_hbm, scale_ref, load_sem.at[1])
    load_b1 = pltpu.make_async_copy(b1_hbm, b1_ref, load_sem.at[2])
    load_b2 = pltpu.make_async_copy(b2_hbm, b2_ref, load_sem.at[2])
    load1 = pltpu.make_async_copy(w1_hbm.at[0], w1, load_sem.at[2])
    load2 = pltpu.make_async_copy(w2_hbm.at[0], w2, load_sem.at[3])

    def load_tok(i):
        return pltpu.make_async_copy(tok_hbm.at[i], tok.at[i], tok_sem.at[i])

    load_keys.start()
    load_scale.start()
    for i in range(images):
        load_tok(i).start()
    barrier = pltpu.get_barrier_semaphore()

    def greet(t, dev):
        pl.semaphore_signal(barrier, inc=1, device_id=dev, device_id_type=MESH)

    for b in near[::-1]:
        for_band(greet, b)

    load_keys.wait()
    slot_of = lax.broadcasted_iota(jnp.int32, (slots, owners), 0) // images
    col = lax.broadcasted_iota(jnp.int32, (slots, owners), 1)
    spread = jnp.where(slot_of == col, 1.0, 0.0).astype(BF16)
    keys = jnp.dot(spread, keys_ref[...], preferred_element_type=F32)
    load_scale.wait()
    key_scale = lax.rsqrt(jnp.mean(keys * keys, axis=1, keepdims=True) + norm_eps)
    key_scale = key_scale * (scale_ref[0] * (LOG2E / width))
    keys = keys.astype(BF16)
    image_of = lax.broadcasted_iota(jnp.int32, (slots, patches), 0) % images

    total = jnp.zeros((slots, width), F32)
    summed = jnp.zeros((slots, patches), F32)
    raw, inv, powers = [], [], []

    def dispatch(i, total, summed):
        power = jnp.exp2(raw[i] * key_scale * inv[i])
        powers.append(power)
        picked = jnp.where(image_of == i, power, 0.0)
        total = total + jnp.dot(
            picked.astype(BF16), tok[i], preferred_element_type=F32
        )
        return total, summed + picked

    for i in range(images):
        load_tok(i).wait()
        t = tok[i]
        raw.append(lax.dot_general(keys, t, NT, preferred_element_type=F32))
        inv.append(lax.rsqrt(row_squares(t) / width + norm_eps))
        if i == images - 1:
            load1.start()
            load2.start()
            load_b1.start()
            load_b2.start()
        if i > 0:
            total, summed = dispatch(i - 1, total, summed)
    total, summed = dispatch(images - 1, total, summed)
    total = total * (1.0 / jnp.sum(summed, axis=1, keepdims=True))
    for n in range(owners):
        send[n] = total[n * images : (n + 1) * images].astype(BF16)

    pl.semaphore_wait(barrier, groups)

    def start_out(t, dev):
        pltpu.make_async_remote_copy(
            src_ref=send.at[lax.div(t, halves)],
            dst_ref=recv.at[core, me],
            send_sem=sent_sem.at[0],
            recv_sem=band_sem.at[band],
            device_id=dev,
            device_id_type=MESH,
        ).start()

    for b in near[::-1]:
        for_band(start_out, b)

    for i in range(images):
        mix = powers[i] * (images / jnp.sum(powers[i], axis=0, keepdims=True))
        comb_ref[i] = jnp.where(image_of == i, mix, 0.0).T.astype(BF16)

    def relay(b):
        block = recv.at[other, pl.ds(b * per, per)]
        return pltpu.make_async_remote_copy(
            src_ref=block,
            dst_ref=block,
            send_sem=sent_sem.at[1],
            recv_sem=land_sem.at[0],
            device_id=partner,
            device_id_type=MESH,
        )

    def whole(ref, send_sem, recv_sem):
        return pltpu.make_async_remote_copy(
            src_ref=ref,
            dst_ref=ref,
            send_sem=send_sem,
            recv_sem=recv_sem,
            device_id=partner,
            device_id_type=MESH,
        )

    for b in near:
        block = recv.at[other, pl.ds(b * per, per)]
        whole(block, sent_sem.at[0], band_sem.at[b]).wait_recv()
        relay(b).start()

    whole(recv.at[0], sent_sem.at[0], land_sem.at[0]).wait_recv()

    for side in range(CORES):

        def place(k, c):
            pairs = [recv[side, 2 * k + q].astype(F32) for q in range(2)]
            at = pl.multiple_of(side * rows + k * 2 * images, 2 * images)
            xf[pl.ds(at, 2 * images), :] = jnp.concatenate(pairs, axis=0)
            return c

        lax.fori_loop(0, groups // 2, place, 0, unroll=groups <= 16)

    load1.wait()
    load_b1.wait()
    load_b2.wait()
    block = min(128, CORES * rows)
    steps = CORES * rows // block

    def first(m, c):
        at = pl.multiple_of(m * block, block)
        x = xf[pl.ds(at, block), :].astype(BF16)
        for j in range(0, hidden, chunk):
            v = jnp.dot(x, w1[:, j : j + chunk], preferred_element_type=F32)
            v = v + b1_ref[0:1, j : j + chunk].astype(F32)
            hid[pl.ds(at, block), j : j + chunk] = erf_gelu(v).astype(BF16)
        return c

    lax.fori_loop(0, steps, first, 0, unroll=steps == 1)
    load2.wait()

    def pair_copy(k):
        lo, hi = cuts[k], cuts[k + 1]
        at = pl.multiple_of(core * rows, rows)
        return pltpu.make_async_remote_copy(
            src_ref=part.at[pl.ds(at, rows), lo:hi],
            dst_ref=pair.at[:, lo:hi],
            send_sem=sent_sem.at[2],
            recv_sem=p_recv.at[k],
            device_id=partner,
            device_id_type=MESH,
        )

    for k in range(len(cuts) - 1):

        def second(m, c):
            at = pl.multiple_of(m * block, block)
            h = hid[pl.ds(at, block), :]
            for j in range(cuts[k], cuts[k + 1], chunk):
                v = jnp.dot(h, w2[:, j : j + chunk], preferred_element_type=F32)
                part[pl.ds(at, block), j : j + chunk] = v.astype(BF16)
                mine[pl.ds(at, block), j : j + chunk] = v
            return c

        lax.fori_loop(0, steps, second, 0, unroll=steps == 1)
        pair_copy(k).start()

    for k in range(len(cuts) - 1):
        lo, hi = cuts[k], cuts[k + 1]
        pair_copy(k).wait_recv()

        def join(q, c):
            at = pl.multiple_of(q * 4 * images, 4 * images)
            own_at = pl.multiple_of(other * rows + at, 4 * images)
            v = mine[pl.ds(own_at, 4 * images), lo:hi]
            v = v + pair[pl.ds(at, 4 * images), lo:hi].astype(F32)
            for r in range(4):
                back[4 * q + r, :, lo:hi] = v[r * images : (r + 1) * images].astype(
                    BF16
                )
            return c

        lax.fori_loop(0, groups // 4, join, 0, unroll=groups <= 16)

    def start_home(t, dev):
        pltpu.make_async_remote_copy(
            src_ref=back.at[t],
            dst_ref=got.at[me],
            send_sem=sent_sem.at[3],
            recv_sem=land_sem.at[1],
            device_id=dev,
            device_id_type=MESH,
        ).start()

    for b in near[::-1]:
        for_band(start_home, b)

    whole(recv.at[0], sent_sem.at[0], land_sem.at[0]).wait_send()
    whole(recv.at[0], sent_sem.at[1], land_sem.at[0]).wait_send()
    for k in range(len(cuts) - 1):
        pair_copy(k).wait_send()
    whole(back, sent_sem.at[3], land_sem.at[1]).wait_send()
    whole(got, sent_sem.at[3], land_sem.at[1]).wait_recv()
    bias = b2_ref[...].astype(F32)
    for n in range(0, owners, 4):
        four = []
        for q in range(n, n + 4):
            v = got[q * halves].astype(F32)
            for x in range(1, halves):
                v = v + got[q * halves + x].astype(F32)
            four.append(v + bias[q : q + 1])
        block = jnp.concatenate(four, axis=0)
        ret_ref[n * images : (n + 4) * images, :] = block.astype(BF16)


def mix_kernel(pieces, comb_ref, ret_ref, out_ref, out, out_sem):
    images, patches, _ = comb_ref.shape
    step = patches // pieces
    ret = ret_ref[...]
    copies = []
    for i in range(images):
        for k in range(pieces):
            at = pl.ds(k * step, step)
            v = jnp.dot(comb_ref[i, at], ret, preferred_element_type=F32)
            out[i, at] = v.astype(out.dtype)
            copies.append(
                pltpu.make_async_copy(out.at[i, at], out_ref.at[i, at], out_sem.at[0])
            )
            copies[-1].start()
    for copy in copies:
        copy.wait()


def body(tokens, slot_keys, logit_scale, up_weight, up_bias, down_weight, down_bias):
    images, patches, width = tokens.shape
    owners = lax.axis_size("expert")
    n_dp = lax.axis_size("dp")
    hidden = up_weight.shape[2]
    halves = n_dp // CORES
    groups = halves * owners
    rows = groups * images
    slots = owners * images
    chunk = 256
    middle = (width // chunk + 1) // 2 * chunk
    cuts = (0, middle, width)
    vmem = pl.BlockSpec(memory_space=pltpu.VMEM)
    hbm = pl.BlockSpec(memory_space=pl.ANY)
    dma = pltpu.SemaphoreType.DMA
    comb, ret = pl.pallas_call(
        functools.partial(route_and_experts, owners, n_dp, chunk, cuts),
        out_shape=(
            pltpu.VMEM((images, patches, slots), BF16),
            pltpu.VMEM((slots, width), BF16),
        ),
        in_specs=[
            hbm,
            hbm,
            pl.BlockSpec(memory_space=pltpu.HBM),
            hbm,
            hbm,
            hbm,
            hbm,
        ],
        out_specs=(vmem, vmem),
        scratch_shapes=[
            pltpu.VMEM((owners, width), BF16),
            pltpu.SMEM((1,), F32),
            pltpu.VMEM(up_bias.shape, BF16),
            pltpu.VMEM(down_bias.shape, BF16),
            pltpu.VMEM((images, patches, width), BF16),
            pltpu.VMEM((width, hidden), BF16),
            pltpu.VMEM((hidden, width), BF16),
            pltpu.VMEM((owners, images, width), BF16),
            pltpu.VMEM((CORES, groups, images, width), BF16),
            pltpu.VMEM((CORES * rows, width), F32),
            pltpu.VMEM((CORES * rows, hidden), BF16),
            pltpu.VMEM((CORES * rows, width), BF16),
            pltpu.VMEM((CORES * rows, width), F32),
            pltpu.VMEM((rows, width), BF16),
            pltpu.VMEM((groups, images, width), BF16),
            pltpu.VMEM((groups, images, width), BF16),
            dma((4,)),
            dma((images,)),
            dma((4,)),
            dma((BANDS,)),
            dma((2,)),
            dma((len(cuts) - 1,)),
        ],
        compiler_params=pltpu.CompilerParams(
            collective_id=0, has_side_effects=True, vmem_limit_bytes=60 * 1024 * 1024
        ),
        name="route_and_experts",
    )(tokens, slot_keys.T, logit_scale, up_weight, up_bias, down_weight, down_bias)
    return pl.pallas_call(
        functools.partial(mix_kernel, 2),
        out_shape=jax.ShapeDtypeStruct(tokens.shape, BF16),
        in_specs=[vmem, vmem],
        out_specs=hbm,
        scratch_shapes=[pltpu.VMEM(tokens.shape, BF16), dma((1,))],
        name="mix_tokens",
    )(
        pltpu.with_memory_space_constraint(comb, pltpu.VMEM),
        pltpu.with_memory_space_constraint(ret, pltpu.VMEM),
    )


def solution(mesh):
    return jax.shard_map(
        body,
        mesh=mesh,
        in_specs=(
            P(("dp", "expert"), None, None),
            P(),
            P(),
            P("expert", None, "dp"),
            P("expert", "dp"),
            P("expert", "dp", None),
            P(),
        ),
        out_specs=P(("dp", "expert"), None, None),
        check_vma=False,
    )
```

time: 26.9 us -> 23.7 us (0.88)
  Pallas kernels: 26 us -> 22.9 us
    pallas_call x2, Pallas kernels: 26 us -> 22.9 us  [the longest x1 21.2 us: body(): pl.pallas_call(functools.partial(route_and_experts, owners, n_dp, chunk,...]
where the time goes in v1:
time: 23.7 us; the launch traced here: 23.6 us
  Pallas kernels  22.9 us (97%)
  between operations  0.66 us (3%)
    pallas_call x1, Pallas kernels, body(): pl.pallas_call(functools.partial(route_and_experts, owners, n_dp, chunk,...  21.2 us
    pallas_call x1, Pallas kernels, body(): pl.pallas_call(functools.partial(mix_kernel, 2), out_shape=jax.ShapeDtype...  1.72 us

profile of v1, /device:TPU:0, one launch (start us, length us, event | category | flops | bytes accessed | tf_op | source)
XLA Modules:
  0.0 23.6 jit_solution(14897421072725209363)
XLA Ops:
  0.7 21.2 %route_and_experts.1 = (bf16[4,256,32]{2,1,0:T(8,128)(2,1)S(1)}, bf16[32,1280]{1,0:T(8,128)(2,1)S(1)}) custom-call(bf16[4,256,1280]{2,1,0:T(8,128)(2,1)} %tok_hbm.1, bf16[8,1280]{1,0:T(8,128)(2,1)} %bitcast.1, f32[1]{0:T(128)S(6)} %copy.8.scale_hbm, bf16[1,1280,1280]{2,1,0:T(8,128)(2,1)} %w1_hbm.1, bf16[1,1280]{1,0:T(2,128)(2,1)} %b1_hbm.1, ...), custom_call_target="tpu_custom_call" | custom-call | tf_op jit(solution)/shard_map/route_and_experts/pallas_call | solution.py:363
  21.9 1.7 %mix_tokens.1 = bf16[4,256,1280]{2,1,0:T(8,128)(2,1)} custom-call(bf16[4,256,32]{2,1,0:T(8,128)(2,1)S(1)} %get-tuple-element.7.comb_ref, bf16[32,1280]{1,0:T(8,128)(2,1)S(1)} %get-tuple-element.8.ret_ref), custom_call_target="tpu_custom_call" | custom-call | tf_op jit(solution)/shard_map/mix_tokens/pallas_call | solution.py:408

commit v2 on v1

--- a/solution.py
+++ b/solution.py
@@ -27,11 +27,18 @@
     for j in range(0, width, 128):
         u = t[:, j : j + 128].astype(F32)
         s = s + u * u
-    hi = s.astype(BF16)
-    lo = (s - hi.astype(F32)).astype(BF16)
-    both = jnp.concatenate([hi, lo], axis=1)
-    ones = jnp.ones((16, 256), BF16)
-    return lax.dot_general(ones, both, NT, preferred_element_type=F32)[0:1]
+    return jnp.sum(s.T, axis=0, keepdims=True)
+
+
+def scores(keys, t):
+    middle = t.shape[0] // 2
+    return jnp.concatenate(
+        [
+            lax.dot_general(keys, u, NT, preferred_element_type=F32)
+            for u in (t[:middle], t[middle:])
+        ],
+        axis=1,
+    )
 
 
 def route_and_experts(
@@ -137,34 +144,38 @@
     for b in near[::-1]:
         for_band(greet, b)
 
-    load_keys.wait()
-    slot_of = lax.broadcasted_iota(jnp.int32, (slots, owners), 0) // images
-    col = lax.broadcasted_iota(jnp.int32, (slots, owners), 1)
-    spread = jnp.where(slot_of == col, 1.0, 0.0).astype(BF16)
-    keys = jnp.dot(spread, keys_ref[...], preferred_element_type=F32)
-    load_scale.wait()
-    key_scale = lax.rsqrt(jnp.mean(keys * keys, axis=1, keepdims=True) + norm_eps)
-    key_scale = key_scale * (scale_ref[0] * (LOG2E / width))
-    keys = keys.astype(BF16)
     image_of = lax.broadcasted_iota(jnp.int32, (slots, patches), 0) % images
-
     total = jnp.zeros((slots, width), F32)
     summed = jnp.zeros((slots, patches), F32)
-    raw, inv, powers = [], [], []
+    raw, inv, shares = [], [], []
 
     def dispatch(i, total, summed):
         power = jnp.exp2(raw[i] * key_scale * inv[i])
-        powers.append(power)
+        share = 1.0 / jnp.sum(power, axis=0, keepdims=True)
+        power = jnp.concatenate(
+            [
+                jnp.broadcast_to(power[n : n + 1], (images, patches))
+                for n in range(owners)
+            ],
+            axis=0,
+        )
         picked = jnp.where(image_of == i, power, 0.0)
+        shares.append(picked * share)
         total = total + jnp.dot(
             picked.astype(BF16), tok[i], preferred_element_type=F32
         )
         return total, summed + picked
 
+    load_keys.wait()
+    load_scale.wait()
+    keys = keys_ref[...]
+    wide = keys.astype(F32)
+    key_scale = lax.rsqrt(jnp.mean(wide * wide, axis=1, keepdims=True) + norm_eps)
+    key_scale = key_scale * (scale_ref[0] * (LOG2E / width))
     for i in range(images):
         load_tok(i).wait()
         t = tok[i]
-        raw.append(lax.dot_general(keys, t, NT, preferred_element_type=F32))
+        raw.append(scores(keys, t))
         inv.append(lax.rsqrt(row_squares(t) / width + norm_eps))
         if i == images - 1:
             load1.start()
@@ -194,8 +205,7 @@
         for_band(start_out, b)
 
     for i in range(images):
-        mix = powers[i] * (images / jnp.sum(powers[i], axis=0, keepdims=True))
-        comb_ref[i] = jnp.where(image_of == i, mix, 0.0).T.astype(BF16)
+        comb_ref[i] = shares[i].T.astype(BF16)
 
     def relay(b):
         block = recv.at[other, pl.ds(b * per, per)]

time: 23.7 us -> 23.1 us (0.975)
  Pallas kernels: 22.9 us -> 22.3 us
    pallas_call x1, Pallas kernels: 21.2 us -> 20.6 us  [body(): pl.pallas_call(functools.partial(route_and_experts, owners, n_dp, chunk,...]
where the time goes in v2:
time: 23.1 us; the launch traced here: 22.9 us
  Pallas kernels  22.3 us (97%)
  between operations  0.66 us (3%)
    pallas_call x1, Pallas kernels, body(): pl.pallas_call(functools.partial(route_and_experts, owners, n_dp, chunk,...  20.6 us
    pallas_call x1, Pallas kernels, body(): pl.pallas_call(functools.partial(mix_kernel, 2), out_shape=jax.ShapeDtype...  1.72 us

profile of v2, /device:TPU:0, one launch (start us, length us, event | category | flops | bytes accessed | tf_op | source)
XLA Modules:
  0.0 22.9 jit_solution(15352638376731551654)
XLA Ops:
  0.7 20.6 %route_and_experts.1 = (bf16[4,256,32]{2,1,0:T(8,128)(2,1)S(1)}, bf16[32,1280]{1,0:T(8,128)(2,1)S(1)}) custom-call(bf16[4,256,1280]{2,1,0:T(8,128)(2,1)} %tok_hbm.1, bf16[8,1280]{1,0:T(8,128)(2,1)} %bitcast.1, f32[1]{0:T(128)S(6)} %copy.8.scale_hbm, bf16[1,1280,1280]{2,1,0:T(8,128)(2,1)} %w1_hbm.1, bf16[1,1280]{1,0:T(2,128)(2,1)} %b1_hbm.1, ...), custom_call_target="tpu_custom_call" | custom-call | tf_op jit(solution)/shard_map/route_and_experts/pallas_call | solution.py:373
  21.2 1.7 %mix_tokens.1 = bf16[4,256,1280]{2,1,0:T(8,128)(2,1)} custom-call(bf16[4,256,32]{2,1,0:T(8,128)(2,1)S(1)} %get-tuple-element.7.comb_ref, bf16[32,1280]{1,0:T(8,128)(2,1)S(1)} %get-tuple-element.8.ret_ref), custom_call_target="tpu_custom_call" | custom-call | tf_op jit(solution)/shard_map/mix_tokens/pallas_call | solution.py:418
